TPU v7x, 32 devices: a whole 2x2x4 slice. The times are simulated.
32 devices in a mesh: groups: 2 (over x), seq: 16 (over z, y, core).
Axes of the slice: x: 2, y: 2, z: 4, core: 2. Of those that a mesh axis runs over, the one named last changes fastest.
Arguments:
- prefill_keys: bfloat16 [128, 4096, 128], P(('groups', 'seq')), parts along dimension 0, may hold values from -4 to 4
- prefill_values: bfloat16 [128, 4096, 128], P(('groups', 'seq')), parts along dimension 0, may hold values from -6 to 6
- window_queries: bfloat16 [128, 8, 256, 128], P(('groups', 'seq')), parts along dimension 0, may hold values from -48 to 48
- step_queries: bfloat16 [128, 2, 8, 128], P('groups'), parts along dimension 0, may hold values from -48 to 48
- new_keys: bfloat16 [128, 2, 128], P('groups'), parts along dimension 0, may hold values from -24 to 24
- new_values: bfloat16 [128, 2, 128], P('groups'), parts along dimension 0, may hold values from -6 to 6
- lengths: int32 [16], P('groups'), parts along dimension 0, may hold values from 2048 to 4096
- keep_mask: int32 [16, 32], P('groups'), parts along dimension 0, may hold values from 0 to 1, as said below
Outputs:
- cache_keys: bfloat16 [128, 4096, 128], P('groups', 'seq'), parts along dimension 0
- cache_values: bfloat16 [128, 4096, 128], P('groups', 'seq'), parts along dimension 0
- attended: bfloat16 [128, 2, 8, 128], P('groups'), parts along dimension 0
- block_scores: float32 [128, 32], P('groups', 'seq'), parts along dimension 0
There are 2 independent parts, one for each index of `groups`. A program takes and returns all parts, laid end to end along the dimension named above; each array names one. Nothing has to cross between parts.
Inputs may be any that keep to these rules, and one draw needn't show every extreme that they name: `keep_mask`: 1 keeps a block, 0 drops it; block 0 of every sequence is kept.
All inputs are finite; a program needn't handle non-finite values.
Results may differ from a plain program's by a relative error of at most 0.0055.
Values may be sent and summed in bfloat16 or wider, within the bound.
A program may use at most 128 MiB of HBM per device.

v0:
```python
import functools
import math

import jax
import jax.numpy as jnp
from jax import lax
from jax.experimental import pallas as pl
from jax.experimental.pallas import tpu as pltpu
from jax.sharding import PartitionSpec as P

KVH = 8
BLOCK = 128
LOW = -1e30
LIMIT = 56 * 1024 * 1024
MESH = pl.DeviceIdType.MESH


def kernel(
    n,
    chunk,
    inner,
    keys_hbm,
    values_hbm,
    window_hbm,
    queries_hbm,
    new_keys_hbm,
    new_values_hbm,
    lengths_hbm,
    keep_hbm,
    cache_keys,
    cache_values,
    attended_out,
    scores_all,
    keys,
    values,
    window,
    queries,
    new_keys,
    new_values,
    lengths_ref,
    keep_ref,
    scaled_queries,
    block_max,
    block_sum,
    mass_acc,
    attended_own,
    scores_own,
    local_sems,
    key_send,
    key_recv,
    value_send,
    value_recv,
    along_send,
    along_recv,
    across_send,
    across_recv,
    score_send,
    score_recv,
):
    group_me = lax.axis_index("groups")
    me = lax.axis_index("seq")
    pairs, tokens, width = keys_hbm.shape
    part = tokens // n
    group = window_hbm.shape[1]
    win = window_hbm.shape[2]
    steps = queries_hbm.shape[1]
    blocks = tokens // BLOCK
    first_pair = me * pairs
    scaling = 1.0 / math.sqrt(width)

    barrier = pltpu.get_barrier_semaphore()
    for k in range(1, n):
        pl.semaphore_signal(
            barrier, inc=1, device_id=(group_me, lax.rem(me + k, n)), device_id_type=MESH
        )

    loads = [
        pltpu.make_async_copy(keys_hbm, keys, local_sems.at[0]),
        pltpu.make_async_copy(values_hbm, values, local_sems.at[1]),
        pltpu.make_async_copy(window_hbm, window, local_sems.at[2]),
        pltpu.make_async_copy(queries_hbm.at[pl.ds(first_pair, pairs)], queries, local_sems.at[3]),
        pltpu.make_async_copy(new_keys_hbm.at[pl.ds(first_pair, pairs)], new_keys, local_sems.at[4]),
        pltpu.make_async_copy(
            new_values_hbm.at[pl.ds(first_pair, pairs)], new_values, local_sems.at[5]
        ),
        pltpu.make_async_copy(
            keys_hbm.at[:, pl.ds(me * part, part), :],
            cache_keys.at[pl.ds(first_pair, pairs)],
            local_sems.at[6],
        ),
        pltpu.make_async_copy(
            values_hbm.at[:, pl.ds(me * part, part), :],
            cache_values.at[pl.ds(first_pair, pairs)],
            local_sems.at[7],
        ),
        pltpu.make_async_copy(lengths_hbm, lengths_ref, local_sems.at[8]),
        pltpu.make_async_copy(keep_hbm, keep_ref, local_sems.at[9]),
    ]
    for load in loads:
        load.start()
    pl.semaphore_wait(barrier, n - 1)

    def remote(src, dst, send, recv, k):
        return pltpu.make_async_remote_copy(
            src_ref=src,
            dst_ref=dst,
            send_sem=send.at[k],
            recv_sem=recv.at[k],
            device_id=(group_me, lax.rem(me + k, n)),
            device_id_type=MESH,
        )

    sends = []
    for src, dst, send, recv in (
        (keys_hbm, cache_keys, key_send, key_recv),
        (values_hbm, cache_values, value_send, value_recv),
    ):
        for k in range(1, n):
            peer = lax.rem(me + k, n)
            sends.append(
                remote(
                    src.at[:, pl.ds(peer * part, part), :],
                    dst.at[pl.ds(first_pair, pairs)],
                    send,
                    recv,
                    k,
                )
            )
    for copy in sends[: n - 1]:
        copy.start()
    for load in loads:
        load.wait()

    lanes = lax.broadcasted_iota(jnp.int32, (1, BLOCK), 1)
    scores_own[...] = jnp.zeros_like(scores_own)

    def decode(p, carry):
        seq_id = (first_pair + p) // KVH
        length = lengths_ref[seq_id]
        rows = queries[p].reshape(steps * group, width)
        scores = (
            lax.dot_general(
                rows, keys[p], (((1,), (1,)), ((), ())), preferred_element_type=jnp.float32
            )
            * scaling
        )
        limits = []
        for b in range(blocks):
            limit = jnp.where(keep_ref[seq_id, b] > 0, length - b * BLOCK, 0)
            limits.append(lanes < limit)
        visible = jnp.concatenate([jnp.where(v, 0.0, -jnp.inf) for v in limits], axis=1)
        scores = scores + visible
        rows32 = rows.astype(jnp.float32)
        row_step = lax.broadcasted_iota(jnp.int32, (steps * group, 1), 0) // group
        own = []
        highest = jnp.max(scores, axis=1, keepdims=True)
        for j in range(steps):
            key_row = new_keys[p, j : j + 1].astype(jnp.float32)
            own_j = jnp.sum(rows32 * key_row, axis=1, keepdims=True) * scaling
            own_j = jnp.where(j <= row_step, own_j, -jnp.inf)
            own.append(own_j)
            highest = jnp.maximum(highest, own_j)
        weights = jnp.exp(scores - highest)
        total = jnp.sum(weights, axis=1, keepdims=True)
        summed = jnp.dot(
            weights.astype(jnp.bfloat16), values[p], preferred_element_type=jnp.float32
        )
        for j in range(steps):
            own_weight = jnp.exp(own[j] - highest)
            total = total + own_weight
            value_row = new_values[p, j : j + 1].astype(jnp.float32)
            summed = summed + own_weight.astype(jnp.bfloat16).astype(jnp.float32) * value_row
        attended_own[p] = (summed / total).astype(jnp.bfloat16).reshape(steps, group, width)
        mass = jnp.sum(weights / total, axis=0, keepdims=True) / group
        line = jnp.zeros((1, BLOCK), jnp.float32)
        for b in range(blocks):
            piece = jnp.sum(mass[:, b * BLOCK : (b + 1) * BLOCK], axis=1, keepdims=True)
            line = line + jnp.where(lanes == b, piece, 0.0)
        scores_own[pl.ds(p, 1), :] = line
        return carry

    lax.fori_loop(0, pairs, decode, 0)

    row, column = me // inner, lax.rem(me, inner)
    rows = n // inner
    along = []
    for i in range(1, rows):
        along.append(
            pltpu.make_async_remote_copy(
                src_ref=attended_own,
                dst_ref=attended_out.at[pl.ds(first_pair, pairs)],
                send_sem=along_send.at[i],
                recv_sem=along_recv.at[i],
                device_id=(group_me, lax.rem(row + i, rows) * inner + column),
                device_id_type=MESH,
            )
        )
    for copy in along:
        copy.start()
    late = len(sends)
    for copy in sends[n - 1 : late]:
        copy.start()

    factor = scaling * math.log2(math.e)
    per_chunk = chunk // BLOCK
    gap = lax.broadcasted_iota(jnp.int32, (BLOCK, win), 1) - lax.broadcasted_iota(
        jnp.int32, (BLOCK, win), 0
    )
    row_block = lax.broadcasted_iota(jnp.int32, (blocks * 8, BLOCK), 0) // 8
    in_block = row_block == lax.broadcasted_iota(jnp.int32, (blocks * 8, BLOCK), 1)

    def one_pair(p, carry):
        seq_id = (first_pair + p) // KVH
        start = lengths_ref[seq_id] - win
        mass_acc[...] = jnp.zeros_like(mass_acc)

        def one_head(g, carry):
            wide = window[p, g].astype(jnp.float32) * factor
            high = wide.astype(jnp.bfloat16)
            low = (wide - high.astype(jnp.float32)).astype(jnp.bfloat16)
            scaled_queries[...] = jnp.concatenate([high.T, low.T], axis=0)

            def one_chunk(c, carry):
                base = pl.multiple_of(c * chunk, chunk)
                tile = keys[p, pl.ds(base, chunk), :]
                doubled = jnp.concatenate([tile, tile], axis=1)
                scores = jnp.dot(doubled, scaled_queries[...], preferred_element_type=jnp.float32)
                for i in range(per_chunk):
                    b = c * per_chunk + i
                    part_scores = jnp.where(
                        gap >= b * BLOCK - start, scores[i * BLOCK : (i + 1) * BLOCK], LOW
                    )
                    stacked = part_scores.reshape(BLOCK // 8, 8, win)
                    top = jnp.max(stacked, axis=0)
                    total = jnp.sum(jnp.exp2(stacked - top[None]), axis=0)
                    kept = keep_ref[seq_id, b] > 0
                    spot = pl.ds(pl.multiple_of(b * 8, 8), 8)
                    block_max[spot, :] = jnp.where(kept, top, LOW)
                    block_sum[spot, :] = jnp.where(kept, total, 0.0)
                return carry

            lax.fori_loop(0, tokens // chunk, one_chunk, 0)
            highest = jnp.max(block_max[...], axis=0, keepdims=True)
            shares = block_sum[...] * jnp.exp2(block_max[...] - highest)
            mass_acc[...] += shares / jnp.sum(shares, axis=0, keepdims=True)
            return carry

        lax.fori_loop(0, group, one_head, 0)
        row_mass = jnp.sum(mass_acc[...], axis=1, keepdims=True)
        prior = jnp.sum(jnp.where(in_block, row_mass, 0.0), axis=0, keepdims=True) / group
        line = prior.astype(jnp.bfloat16).astype(jnp.float32)
        scores_own[pl.ds(p, 1), :] = scores_own[pl.ds(p, 1), :] + line
        return carry

    lax.fori_loop(0, pairs, one_pair, 0)

    small = [
        remote(scores_own, scores_all.at[me], score_send, score_recv, k) for k in range(1, n)
    ]
    for copy in small:
        copy.start()
    for copy in along:
        copy.wait()
    across = []
    for i in range(rows):
        source = lax.rem(row + rows - i, rows) * inner + column
        spot = pl.ds(source * pairs, pairs)
        for j in range(1, inner):
            across.append(
                pltpu.make_async_remote_copy(
                    src_ref=attended_own if i == 0 else attended_out.at[spot],
                    dst_ref=attended_out.at[spot],
                    send_sem=across_send.at[i * inner + j],
                    recv_sem=across_recv.at[i * inner + j],
                    device_id=(group_me, row * inner + lax.rem(column + j, inner)),
                    device_id_type=MESH,
                )
            )
    for copy in across:
        copy.start()
    for copy in sends[late:]:
        copy.start()
    kept_here = [
        pltpu.make_async_copy(
            attended_own, attended_out.at[pl.ds(first_pair, pairs)], local_sems.at[0]
        ),
        pltpu.make_async_copy(scores_own, scores_all.at[me], local_sems.at[1]),
    ]
    for copy in kept_here:
        copy.start()
    for copy in kept_here:
        copy.wait()
    for copy in small:
        copy.wait()
    for copy in across:
        copy.wait()
    for copy in sends:
        copy.wait()


def settle(n, pieces, keys_in, values_in, attended_in, scores_in, *rest):
    cache_keys, cache_values, attended_out, scores_out = rest[:4]
    keys, values, attended, scores, sems = rest[4:]
    me = lax.axis_index("seq")
    here = scores_out.shape[0]
    step = keys_in.shape[0] // pieces
    chunks = []
    for source, middle, target in ((keys_in, keys, cache_keys), (values_in, values, cache_values)):
        for i in range(pieces):
            spot = pl.ds(i * step, step)
            chunks.append((source.at[spot], middle.at[spot], target.at[spot]))
    chunks.append((attended_in, attended, attended_out))
    loads = [pltpu.make_async_copy(c[0], c[1], sems.at[0, i]) for i, c in enumerate(chunks)]
    stores = [pltpu.make_async_copy(c[1], c[2], sems.at[1, i]) for i, c in enumerate(chunks)]
    score_load = pltpu.make_async_copy(scores_in, scores, sems.at[0, len(chunks)])
    score_load.start()
    for load in loads:
        load.start()
    score_load.wait()
    flat = scores[...].reshape(scores.shape[0] * scores.shape[1], BLOCK)
    turned = pltpu.roll(flat, lax.rem(BLOCK - me * here, BLOCK), 1)
    scores_out[...] = turned.T[:here]
    for load, store in zip(loads, stores):
        load.wait()
        store.start()
    for store in stores:
        store.wait()


def local(n, *args):
    keys, values, window, queries, new_keys, new_values, lengths, keep = args
    pairs, tokens, width = keys.shape
    part = tokens // n
    blocks = tokens // BLOCK
    win = window.shape[2]
    every = n * pairs
    inner = 4 if n % 4 == 0 else 1
    vmem = pl.BlockSpec(memory_space=pltpu.VMEM)
    hbm = pl.BlockSpec(memory_space=pltpu.HBM)
    free = pl.BlockSpec(memory_space=pl.ANY)
    bf16, f32 = jnp.bfloat16, jnp.float32
    moved = pl.pallas_call(
        functools.partial(kernel, n, min(512, tokens), inner),
        out_shape=(
            jax.ShapeDtypeStruct((every, part, width), bf16),
            jax.ShapeDtypeStruct((every, part, width), bf16),
            jax.ShapeDtypeStruct((every,) + queries.shape[1:], bf16),
            jax.ShapeDtypeStruct((n, pairs, BLOCK), f32),
        ),
        in_specs=[hbm] * 8,
        out_specs=(free,) * 4,
        scratch_shapes=[
            pltpu.VMEM(keys.shape, bf16),
            pltpu.VMEM(values.shape, bf16),
            pltpu.VMEM(window.shape, bf16),
            pltpu.VMEM((pairs,) + queries.shape[1:], bf16),
            pltpu.VMEM((pairs,) + new_keys.shape[1:], bf16),
            pltpu.VMEM((pairs,) + new_values.shape[1:], bf16),
            pltpu.SMEM(lengths.shape, jnp.int32),
            pltpu.SMEM(keep.shape, jnp.int32),
            pltpu.VMEM((2 * width, win), bf16),
            pltpu.VMEM((blocks * 8, win), f32),
            pltpu.VMEM((blocks * 8, win), f32),
            pltpu.VMEM((blocks * 8, win), f32),
            pltpu.VMEM((pairs,) + queries.shape[1:], bf16),
            pltpu.VMEM((pairs, BLOCK), f32),
            pltpu.SemaphoreType.DMA((10,)),
        ]
        + [pltpu.SemaphoreType.DMA((n,))] * 10,
        compiler_params=pltpu.CompilerParams(
            collective_id=0, has_side_effects=True, vmem_limit_bytes=LIMIT
        ),
    )(*args)
    pieces = math.gcd(every, 8)
    cache_keys, cache_values, attended, scores = pl.pallas_call(
        functools.partial(settle, n, pieces),
        out_shape=(
            jax.ShapeDtypeStruct((every, part, width), bf16),
            jax.ShapeDtypeStruct((every, part, width), bf16),
            jax.ShapeDtypeStruct((every,) + queries.shape[1:], bf16),
            jax.ShapeDtypeStruct((part // BLOCK, every), f32),
        ),
        in_specs=[free] * 4,
        out_specs=(free, free, free, vmem),
        scratch_shapes=[
            pltpu.VMEM((every, part, width), bf16),
            pltpu.VMEM((every, part, width), bf16),
            pltpu.VMEM((every,) + queries.shape[1:], bf16),
            pltpu.VMEM((n, pairs, BLOCK), f32),
            pltpu.SemaphoreType.DMA((2, 2 * pieces + 2)),
        ],
        compiler_params=pltpu.CompilerParams(vmem_limit_bytes=LIMIT),
    )(*moved)
    return cache_keys, cache_values, attended, scores.T


def solution(mesh):
    placed = (
        P(("groups", "seq"), None, None),
        P(("groups", "seq"), None, None),
        P(("groups", "seq"), None, None, None),
        P("groups", None, None, None),
        P("groups", None, None),
        P("groups", None, None),
        P("groups"),
        P("groups", None),
    )
    return jax.shard_map(
        functools.partial(local, mesh.shape["seq"]),
        mesh=mesh,
        in_specs=placed,
        out_specs=(
            P("groups", "seq", None),
            P("groups", "seq", None),
            P("groups", None, None, None),
            P("groups", "seq"),
        ),
        check_vma=False,
    )
```

profile of v0, /device:TPU:19, one launch (start us, length us, event | category | flops | bytes accessed | tf_op | source)
XLA Modules:
  0.0 197.1 jit_solution(17529788683263639167)
XLA Ops:
  0.6 189.1 %shard_map.111 = (bf16[64,256,128]{2,1,0:T(8,128)(2,1)}, bf16[64,256,128]{2,1,0:T(8,128)(2,1)}, bf16[64,2,8,128]{3,2,1,0:T(8,128)(2,1)}, f32[16,4,128]{2,1,0:T(4,128)}) custom-call(bf16[4,4096,128]{2,1,0:T(8,128)(2,1)} %keys_hbm.1, bf16[4,4096,128]{2,1,0:T(8,128)(2,1)} %values_hbm.1, bf16[4,8,256,128]{3,2,1,0:T(8,128)(2,1)} %window_hbm.1, ...), custom_call_target="tpu_custom_call" | custom-call | tf_op jit(solution)/shard_map/pallas_call | solution.py:342
  189.8 7.3 %shard_map.112 = (bf16[64,256,128]{2,1,0:T(8,128)(2,1)}, bf16[64,256,128]{2,1,0:T(8,128)(2,1)}, bf16[64,2,8,128]{3,2,1,0:T(8,128)(2,1)}, f32[2,64]{1,0:T(2,128)}) custom-call(bf16[64,256,128]{2,1,0:T(8,128)(2,1)} %get-tuple-element.12.keys_in, bf16[64,256,128]{2,1,0:T(8,128)(2,1)} %get-tuple-element.13.values_in, ...), custom_call_target="tpu_custom_call" | custom-call | tf_op jit(solution)/shard_map/pallas_call | solution.py:375
where the time goes:
time: 200 us; the launch traced here: 197 us
  Pallas kernels  196 us (98%)
    pallas_call x1, Pallas kernels, local(): pl.pallas_call(functools.partial(kernel, n, min(512, tokens), inner), out...  189 us
    pallas_call x1, Pallas kernels, local(): pl.pallas_call(functools.partial(settle, n, pieces), out_shape=(jax.Shape...  7.33 us

commit v1 on v0

--- a/solution.py
+++ b/solution.py
@@ -11,7 +11,7 @@
 KVH = 8
 BLOCK = 128
 LOW = -1e30
-LIMIT = 56 * 1024 * 1024
+LIMIT = 32 * 1024 * 1024
 MESH = pl.DeviceIdType.MESH
 
 
@@ -298,31 +298,24 @@
         copy.wait()
 
 
-def settle(n, pieces, keys_in, values_in, attended_in, scores_in, *rest):
-    cache_keys, cache_values, attended_out, scores_out = rest[:4]
-    keys, values, attended, scores, sems = rest[4:]
+def settle(n, pieces, keys, values, attended, scores, *rest):
+    cache_keys, cache_values, attended_out, scores_out, sems = rest
     me = lax.axis_index("seq")
     here = scores_out.shape[0]
-    step = keys_in.shape[0] // pieces
-    chunks = []
-    for source, middle, target in ((keys_in, keys, cache_keys), (values_in, values, cache_values)):
+    step = keys.shape[0] // pieces
+    stores = []
+    for source, target in ((keys, cache_keys), (values, cache_values)):
         for i in range(pieces):
             spot = pl.ds(i * step, step)
-            chunks.append((source.at[spot], middle.at[spot], target.at[spot]))
-    chunks.append((attended_in, attended, attended_out))
-    loads = [pltpu.make_async_copy(c[0], c[1], sems.at[0, i]) for i, c in enumerate(chunks)]
-    stores = [pltpu.make_async_copy(c[1], c[2], sems.at[1, i]) for i, c in enumerate(chunks)]
-    score_load = pltpu.make_async_copy(scores_in, scores, sems.at[0, len(chunks)])
-    score_load.start()
-    for load in loads:
-        load.start()
-    score_load.wait()
+            stores.append(
+                pltpu.make_async_copy(source.at[spot], target.at[spot], sems.at[len(stores)])
+            )
+    stores.append(pltpu.make_async_copy(attended, attended_out, sems.at[len(stores)]))
+    for store in stores:
+        store.start()
     flat = scores[...].reshape(scores.shape[0] * scores.shape[1], BLOCK)
     turned = pltpu.roll(flat, lax.rem(BLOCK - me * here, BLOCK), 1)
     scores_out[...] = turned.T[:here]
-    for load, store in zip(loads, stores):
-        load.wait()
-        store.start()
     for store in stores:
         store.wait()
 
@@ -342,13 +335,13 @@
     moved = pl.pallas_call(
         functools.partial(kernel, n, min(512, tokens), inner),
         out_shape=(
-            jax.ShapeDtypeStruct((every, part, width), bf16),
-            jax.ShapeDtypeStruct((every, part, width), bf16),
-            jax.ShapeDtypeStruct((every,) + queries.shape[1:], bf16),
-            jax.ShapeDtypeStruct((n, pairs, BLOCK), f32),
+            pltpu.VMEM((every, part, width), bf16),
+            pltpu.VMEM((every, part, width), bf16),
+            pltpu.VMEM((every,) + queries.shape[1:], bf16),
+            pltpu.VMEM((n, pairs, BLOCK), f32),
         ),
         in_specs=[hbm] * 8,
-        out_specs=(free,) * 4,
+        out_specs=(vmem,) * 4,
         scratch_shapes=[
             pltpu.VMEM(keys.shape, bf16),
             pltpu.VMEM(values.shape, bf16),
@@ -370,7 +363,7 @@
         compiler_params=pltpu.CompilerParams(
             collective_id=0, has_side_effects=True, vmem_limit_bytes=LIMIT
         ),
-    )(*args)
+    )(*(pltpu.with_memory_space_constraint(a, pltpu.HBM) for a in args))
     pieces = math.gcd(every, 8)
     cache_keys, cache_values, attended, scores = pl.pallas_call(
         functools.partial(settle, n, pieces),
@@ -380,15 +373,9 @@
             jax.ShapeDtypeStruct((every,) + queries.shape[1:], bf16),
             jax.ShapeDtypeStruct((part // BLOCK, every), f32),
         ),
-        in_specs=[free] * 4,
+        in_specs=[vmem] * 4,
         out_specs=(free, free, free, vmem),
-        scratch_shapes=[
-            pltpu.VMEM((every, part, width), bf16),
-            pltpu.VMEM((every, part, width), bf16),
-            pltpu.VMEM((every,) + queries.shape[1:], bf16),
-            pltpu.VMEM((n, pairs, BLOCK), f32),
-            pltpu.SemaphoreType.DMA((2, 2 * pieces + 2)),
-        ],
+        scratch_shapes=[pltpu.SemaphoreType.DMA((2 * pieces + 1,))],
         compiler_params=pltpu.CompilerParams(vmem_limit_bytes=LIMIT),
     )(*moved)
     return cache_keys, cache_values, attended, scores.T

time: 200 us -> 196 us (0.980)
  Pallas kernels: 196 us -> 193 us
    pallas_call x1, Pallas kernels: 7.33 us -> 4.06 us  [local(): pl.pallas_call(functools.partial(settle, n, pieces), out_shape=(jax.Shape...]
where the time goes in v1:
time: 196 us; the launch traced here: 194 us
  Pallas kernels  193 us (98%)
    pallas_call x1, Pallas kernels, local(): pl.pallas_call(functools.partial(kernel, n, min(512, tokens), inner), out...  189 us
    pallas_call x1, Pallas kernels, local(): pl.pallas_call(functools.partial(settle, n, pieces), out_shape=(jax.Shape...  4.06 us

profile of v1, /device:TPU:19, one launch (start us, length us, event | category | flops | bytes accessed | tf_op | source)
XLA Modules:
  0.0 193.8 jit_solution(17829697058932875825)
XLA Ops:
  0.6 189.1 %shard_map.111 = (bf16[64,256,128]{2,1,0:T(8,128)(2,1)S(1)}, bf16[64,256,128]{2,1,0:T(8,128)(2,1)S(1)}, bf16[64,2,8,128]{3,2,1,0:T(8,128)(2,1)S(1)}, f32[16,4,128]{2,1,0:T(4,128)S(1)}) custom-call(bf16[4,4096,128]{2,1,0:T(8,128)(2,1)} %keys_hbm.1, bf16[4,4096,128]{2,1,0:T(8,128)(2,1)} %values_hbm.1, bf16[4,8,256,128]{3,2,1,0:T(8,128)(2,1)} %window_hbm.1, ...), custom_call_target="tpu_custom_call" | custom-call | tf_op jit(solution)/shard_map/pallas_call | solution.py:335
  189.7 4.1 %shard_map.112 = (bf16[64,256,128]{2,1,0:T(8,128)(2,1)}, bf16[64,256,128]{2,1,0:T(8,128)(2,1)}, bf16[64,2,8,128]{3,2,1,0:T(8,128)(2,1)}, f32[2,64]{1,0:T(2,128)}) custom-call(bf16[64,256,128]{2,1,0:T(8,128)(2,1)S(1)} %get-tuple-element.12.keys, bf16[64,256,128]{2,1,0:T(8,128)(2,1)S(1)} %get-tuple-element.13.values, ...), custom_call_target="tpu_custom_call" | custom-call | tf_op jit(solution)/shard_map/pallas_call | solution.py:368

commit v2 on v1

--- a/solution.py
+++ b/solution.py
@@ -46,16 +46,19 @@
     attended_own,
     scores_own,
     local_sems,
-    key_send,
-    key_recv,
-    value_send,
-    value_recv,
+    present,
+    up_send,
+    up_recv,
+    down_send,
+    down_recv,
+    near_send,
+    near_recv,
     along_send,
     along_recv,
+    relay_send,
+    relay_recv,
     across_send,
     across_recv,
-    score_send,
-    score_recv,
 ):
     group_me = lax.axis_index("groups")
     me = lax.axis_index("seq")
@@ -67,12 +70,17 @@
     blocks = tokens // BLOCK
     first_pair = me * pairs
     scaling = 1.0 / math.sqrt(width)
+    rows = n // inner
+    row, column = me // inner, lax.rem(me, inner)
 
     barrier = pltpu.get_barrier_semaphore()
     for k in range(1, n):
-        pl.semaphore_signal(
-            barrier, inc=1, device_id=(group_me, lax.rem(me + k, n)), device_id_type=MESH
-        )
+
+        @pl.when(me + k < n)
+        def _():
+            pl.semaphore_signal(
+                barrier, inc=1, device_id=(group_me, me + k), device_id_type=MESH
+            )
 
     loads = [
         pltpu.make_async_copy(keys_hbm, keys, local_sems.at[0]),
@@ -96,38 +104,123 @@
         pltpu.make_async_copy(lengths_hbm, lengths_ref, local_sems.at[8]),
         pltpu.make_async_copy(keep_hbm, keep_ref, local_sems.at[9]),
     ]
+
+    @pl.when(me > 0)
+    def _():
+        pl.semaphore_wait(barrier, me)
+
+    for k in range(1, n):
+
+        @pl.when(me >= k)
+        def _():
+            pl.semaphore_signal(
+                present.at[me], inc=1, device_id=(group_me, me - k), device_id_type=MESH
+            )
+
+    if inner == 4:
+        flip = 2 * lax.rem(column, 2)
+        turns = [flip, 2 - flip, 1 + flip, 3 - flip]
+    else:
+        turns = list(range(inner))
+
+    def move(which, target, spot, send, recv):
+        src, dst = ((keys_hbm, cache_keys), (values_hbm, cache_values))[which]
+        return pltpu.make_async_remote_copy(
+            src_ref=src.at[:, pl.ds(target * part, part), :],
+            dst_ref=dst.at[pl.ds(first_pair, pairs)],
+            send_sem=send.at[which, spot],
+            recv_sem=recv.at[which, spot],
+            device_id=(group_me, target),
+            device_id_type=MESH,
+        )
+
+    def down(which, distance, c):
+        target = lax.rem(row - distance + rows, rows) * inner + (column ^ c)
+        return move(which, target, distance * inner + c, down_send, down_recv)
+
+    def up(which, distance, c):
+        target = lax.rem(row + distance, rows) * inner + (column ^ c)
+        return move(which, target, distance * inner + c, up_send, up_recv)
+
+    def near(which, c):
+        return move(which, row * inner + (column ^ c), c, near_send, near_recv)
+
+    def start_down(distance, kinds):
+        for which in kinds:
+            for c in turns:
+                down(which, distance, c).start()
+
+    def start_up(distance, kinds):
+        for which in kinds:
+            for c in turns:
+                up(which, distance, c).start()
+
+    def await_up(distance, c):
+        pl.semaphore_wait(present.at[(row + distance) * inner + (column ^ c)], 1)
+
+    @pl.when(row > 0)
+    def _():
+        start_down(row, (0, 1))
+
+    for u in range(1, rows - 1):
+
+        @pl.when(u < row - 1)
+        def _():
+            start_down(u, (0, 1))
+
+        @pl.when(u == row - 1)
+        def _():
+            start_down(u, (0,))
+
+    early = [2 * (column // 2) ^ c for c in range(inner)] if inner == 4 else list(range(inner))
+    for u in range(1, rows):
+
+        @pl.when(row + u < rows)
+        def _():
+            for c in early:
+                await_up(u, c)
+                if u > 1:
+                    up(0, u, c).start()
+                else:
+
+                    @pl.when(row > 0)
+                    def _():
+                        up(0, u, c).start()
+
+        if u > 1:
+
+            @pl.when((row == 0) & (row + u < rows))
+            def _():
+                start_up(u, (1,))
+
     for load in loads:
         load.start()
-    pl.semaphore_wait(barrier, n - 1)
-
-    def remote(src, dst, send, recv, k):
-        return pltpu.make_async_remote_copy(
-            src_ref=src,
-            dst_ref=dst,
-            send_sem=send.at[k],
-            recv_sem=recv.at[k],
-            device_id=(group_me, lax.rem(me + k, n)),
-            device_id_type=MESH,
-        )
-
-    sends = []
-    for src, dst, send, recv in (
-        (keys_hbm, cache_keys, key_send, key_recv),
-        (values_hbm, cache_values, value_send, value_recv),
-    ):
-        for k in range(1, n):
-            peer = lax.rem(me + k, n)
-            sends.append(
-                remote(
-                    src.at[:, pl.ds(peer * part, part), :],
-                    dst.at[pl.ds(first_pair, pairs)],
-                    send,
-                    recv,
-                    k,
-                )
-            )
-    for copy in sends[: n - 1]:
-        copy.start()
+    for c in range(1, inner):
+
+        @pl.when((column ^ c) > column)
+        def _():
+            pl.semaphore_wait(present.at[row * inner + (column ^ c)], 1)
+
+        for which in (0, 1):
+            near(which, c).start()
+
+    def start_rest():
+        @pl.when(row > 1)
+        def _():
+            start_down(row - 1, (1,))
+
+        for u in range(rows - 1, 0, -1):
+
+            @pl.when((row > 0) & (row + u < rows))
+            def _():
+                start_up(u, (1,))
+
+        if rows > 1:
+
+            @pl.when(row == 0)
+            def _():
+                start_up(1, (0, 1))
+
     for load in loads:
         load.wait()
 
@@ -181,26 +274,6 @@
 
     lax.fori_loop(0, pairs, decode, 0)
 
-    row, column = me // inner, lax.rem(me, inner)
-    rows = n // inner
-    along = []
-    for i in range(1, rows):
-        along.append(
-            pltpu.make_async_remote_copy(
-                src_ref=attended_own,
-                dst_ref=attended_out.at[pl.ds(first_pair, pairs)],
-                send_sem=along_send.at[i],
-                recv_sem=along_recv.at[i],
-                device_id=(group_me, lax.rem(row + i, rows) * inner + column),
-                device_id_type=MESH,
-            )
-        )
-    for copy in along:
-        copy.start()
-    late = len(sends)
-    for copy in sends[n - 1 : late]:
-        copy.start()
-
     factor = scaling * math.log2(math.e)
     per_chunk = chunk // BLOCK
     gap = lax.broadcasted_iota(jnp.int32, (BLOCK, win), 1) - lax.broadcasted_iota(
@@ -254,48 +327,124 @@
 
     lax.fori_loop(0, pairs, one_pair, 0)
 
-    small = [
-        remote(scores_own, scores_all.at[me], score_send, score_recv, k) for k in range(1, n)
+    results = ((attended_own, attended_out), (scores_own, scores_all))
+    half = rows // 2
+    low = row < half
+
+    def along(i, u):
+        own, landing = results[i]
+        return pltpu.make_async_remote_copy(
+            src_ref=own,
+            dst_ref=landing.at[row, column],
+            send_sem=along_send.at[i, u],
+            recv_sem=along_recv.at[i, u],
+            device_id=(group_me, lax.rem(row + u, rows) * inner + column),
+            device_id_type=MESH,
+        )
+
+    def relay(i, upward, target):
+        landing = results[i][1]
+        block = landing.at[pl.ds(0, half) if upward else pl.ds(half, rows - half), column]
+        return pltpu.make_async_remote_copy(
+            src_ref=block,
+            dst_ref=block,
+            send_sem=relay_send.at[i, target],
+            recv_sem=relay_recv.at[i],
+            device_id=(group_me, target * inner + column),
+            device_id_type=MESH,
+        )
+
+    across = [
+        pltpu.make_async_remote_copy(
+            src_ref=landing.at[:, column],
+            dst_ref=landing.at[:, column],
+            send_sem=across_send.at[i, c],
+            recv_sem=across_recv.at[i, c],
+            device_id=(group_me, row * inner + (column ^ c)),
+            device_id_type=MESH,
+        )
+        for c in range(1, inner)
+        for i, (own, landing) in enumerate(results)
     ]
-    for copy in small:
-        copy.start()
-    for copy in along:
-        copy.wait()
-    across = []
-    for i in range(rows):
-        source = lax.rem(row + rows - i, rows) * inner + column
-        spot = pl.ds(source * pairs, pairs)
-        for j in range(1, inner):
-            across.append(
-                pltpu.make_async_remote_copy(
-                    src_ref=attended_own if i == 0 else attended_out.at[spot],
-                    dst_ref=attended_out.at[spot],
-                    send_sem=across_send.at[i * inner + j],
-                    recv_sem=across_recv.at[i * inner + j],
-                    device_id=(group_me, row * inner + lax.rem(column + j, inner)),
-                    device_id_type=MESH,
-                )
-            )
-    for copy in across:
-        copy.start()
-    for copy in sends[late:]:
-        copy.start()
     kept_here = [
-        pltpu.make_async_copy(
-            attended_own, attended_out.at[pl.ds(first_pair, pairs)], local_sems.at[0]
-        ),
-        pltpu.make_async_copy(scores_own, scores_all.at[me], local_sems.at[1]),
+        pltpu.make_async_copy(own, landing.at[row, column], local_sems.at[i])
+        for i, (own, landing) in enumerate(results)
     ]
+    for u in range(1, rows):
+        target = lax.rem(row + u, rows)
+
+        @pl.when((low == (target < half)) | (target == jnp.where(low, half, half - 1)))
+        def _():
+            for i in range(2):
+                along(i, u).start()
+
+    start_rest()
     for copy in kept_here:
         copy.start()
     for copy in kept_here:
         copy.wait()
-    for copy in small:
-        copy.wait()
+    for u in range(1, rows):
+        source = lax.rem(row + rows - u, rows)
+
+        @pl.when((low == (source < half)) | (row == jnp.where(source < half, half, half - 1)))
+        def _():
+            for i in range(2):
+                along(i, u).wait_recv()
+
+    upper, lower = range(half + 1, rows), range(0, half - 1)
+    for upward, gate, targets in ((True, half, upper), (False, half - 1, lower)):
+        for target in targets:
+
+            @pl.when(row == gate)
+            def _():
+                for i in range(2):
+                    relay(i, upward, target).start()
+
+            @pl.when(row == target)
+            def _():
+                for i in range(2):
+                    relay(i, upward, target).wait_recv()
+
+    for copy in across:
+        copy.start()
     for copy in across:
         copy.wait()
-    for copy in sends:
-        copy.wait()
+    for upward, gate, targets in ((True, half, upper), (False, half - 1, lower)):
+        for target in targets:
+
+            @pl.when(row == gate)
+            def _():
+                for i in range(2):
+                    relay(i, upward, target).wait_send()
+
+    for u in range(1, rows):
+        target = lax.rem(row + u, rows)
+
+        @pl.when((low == (target < half)) | (target == jnp.where(low, half, half - 1)))
+        def _():
+            for i in range(2):
+                along(i, u).wait_send()
+
+    for c in range(1, inner):
+        for which in (0, 1):
+            near(which, c).wait()
+    for u in range(1, rows):
+        for make, sends, receives in (
+            (down, row >= u, row + u < rows),
+            (up, row + u < rows, row >= u),
+        ):
+
+            @pl.when(sends)
+            def _():
+                for which in (0, 1):
+                    for c in range(inner):
+                        make(which, u, c).wait_send()
+
+            @pl.when(receives)
+            def _():
+                for which in (0, 1):
+                    for c in range(inner):
+                        make(which, u, c).wait_recv()
 
 
 def settle(n, pieces, keys, values, attended, scores, *rest):
@@ -313,7 +462,7 @@
     stores.append(pltpu.make_async_copy(attended, attended_out, sems.at[len(stores)]))
     for store in stores:
         store.start()
-    flat = scores[...].reshape(scores.shape[0] * scores.shape[1], BLOCK)
+    flat = scores[...].reshape(math.prod(scores.shape[:-1]), BLOCK)
     turned = pltpu.roll(flat, lax.rem(BLOCK - me * here, BLOCK), 1)
     scores_out[...] = turned.T[:here]
     for store in stores:
@@ -337,8 +486,8 @@
         out_shape=(
             pltpu.VMEM((every, part, width), bf16),
             pltpu.VMEM((every, part, width), bf16),
-            pltpu.VMEM((every,) + queries.shape[1:], bf16),
-            pltpu.VMEM((n, pairs, BLOCK), f32),
+            pltpu.VMEM((n // inner, inner, pairs) + queries.shape[1:], bf16),
+            pltpu.VMEM((n // inner, inner, pairs, BLOCK), f32),
         ),
         in_specs=[hbm] * 8,
         out_specs=(vmem,) * 4,
@@ -359,7 +508,12 @@
             pltpu.VMEM((pairs, BLOCK), f32),
             pltpu.SemaphoreType.DMA((10,)),
         ]
-        + [pltpu.SemaphoreType.DMA((n,))] * 10,
+        + [pltpu.SemaphoreType.REGULAR((n,))]
+        + [pltpu.SemaphoreType.DMA((2, n))] * 4
+        + [pltpu.SemaphoreType.DMA((2, inner))] * 2
+        + [pltpu.SemaphoreType.DMA((2, n))] * 3
+        + [pltpu.SemaphoreType.DMA((2,))]
+        + [pltpu.SemaphoreType.DMA((2, n))] * 2,
         compiler_params=pltpu.CompilerParams(
             collective_id=0, has_side_effects=True, vmem_limit_bytes=LIMIT
         ),
@@ -370,7 +524,7 @@
         out_shape=(
             jax.ShapeDtypeStruct((every, part, width), bf16),
             jax.ShapeDtypeStruct((every, part, width), bf16),
-            jax.ShapeDtypeStruct((every,) + queries.shape[1:], bf16),
+            jax.ShapeDtypeStruct(moved[2].shape, bf16),
             jax.ShapeDtypeStruct((part // BLOCK, every), f32),
         ),
         in_specs=[vmem] * 4,
@@ -378,7 +532,7 @@
         scratch_shapes=[pltpu.SemaphoreType.DMA((2 * pieces + 1,))],
         compiler_params=pltpu.CompilerParams(vmem_limit_bytes=LIMIT),
     )(*moved)
-    return cache_keys, cache_values, attended, scores.T
+    return cache_keys, cache_values, attended.reshape((every,) + queries.shape[1:]), scores.T
 
 
 def solution(mesh):

time: 196 us -> 194 us (0.990)
  no operation moved by 1% of the time
where the time goes in v2:
time: 194 us
  Pallas kernels  193 us (99%)
    pallas_call x1, Pallas kernels, local(): pl.pallas_call(functools.partial(kernel, n, min(512, tokens), inner), out...  189 us
    pallas_call x1, Pallas kernels, local(): pl.pallas_call(functools.partial(settle, n, pieces), out_shape=(jax.Shape...  4.06 us

profile of v2, /device:TPU:19, one launch (start us, length us, event | category | flops | bytes accessed | tf_op | source)
XLA Modules:
  0.0 193.7 jit_solution(1780184091330325198)
XLA Ops:
  0.6 189.0 %shard_map.111 = (bf16[64,256,128]{2,1,0:T(8,128)(2,1)S(1)}, bf16[64,256,128]{2,1,0:T(8,128)(2,1)S(1)}, bf16[4,4,4,2,8,128]{5,4,3,2,1,0:T(8,128)(2,1)S(1)}, f32[4,4,4,128]{3,2,1,0:T(4,128)S(1)}) custom-call(bf16[4,4096,128]{2,1,0:T(8,128)(2,1)} %keys_hbm.1, bf16[4,4096,128]{2,1,0:T(8,128)(2,1)} %values_hbm.1, bf16[4,8,256,128]{3,2,1,0:T(8,128)(2,1)} %window_hbm.1, ...), custom_call_target="tpu_custom_call" | custom-call | tf_op jit(solution)/shard_map/pallas_call | solution.py:484
  189.6 4.1 %shard_map.112 = (bf16[64,256,128]{2,1,0:T(8,128)(2,1)}, bf16[64,256,128]{2,1,0:T(8,128)(2,1)}, bf16[4,4,4,2,8,128]{5,4,3,2,1,0:T(8,128)(2,1)}, f32[2,64]{1,0:T(2,128)}) custom-call(bf16[64,256,128]{2,1,0:T(8,128)(2,1)S(1)} %get-tuple-element.12.keys, bf16[64,256,128]{2,1,0:T(8,128)(2,1)S(1)} %get-tuple-element.13.values, ...), custom_call_target="tpu_custom_call" | custom-call | tf_op jit(solution)/shard_map/pallas_call | solution.py:522

commit v3 on v2

--- a/solution.py
+++ b/solution.py
@@ -73,6 +73,8 @@
     rows = n // inner
     row, column = me // inner, lax.rem(me, inner)
 
+    half = rows // 2
+    gate_low, gate_high = half - 1, half
     barrier = pltpu.get_barrier_semaphore()
     for k in range(1, n):
 
@@ -104,14 +106,26 @@
         pltpu.make_async_copy(lengths_hbm, lengths_ref, local_sems.at[8]),
         pltpu.make_async_copy(keep_hbm, keep_ref, local_sems.at[9]),
     ]
-
-    @pl.when(me > 0)
+    if rows > 1:
+
+        @pl.when(row == gate_high)
+        def _():
+            for c in range(inner):
+                pl.semaphore_signal(
+                    barrier, inc=1, device_id=(group_me, gate_low * inner + c), device_id_type=MESH
+                )
+
+        @pl.when(row == gate_low)
+        def _():
+            pl.semaphore_wait(barrier, me + inner)
+
+    @pl.when((me > 0) & (row != gate_low))
     def _():
         pl.semaphore_wait(barrier, me)
 
     for k in range(1, n):
 
-        @pl.when(me >= k)
+        @pl.when((me >= k) & ((row != gate_high) | ((me - k) // inner != gate_low)))
         def _():
             pl.semaphore_signal(
                 present.at[me], inc=1, device_id=(group_me, me - k), device_id_type=MESH
@@ -178,7 +192,14 @@
         @pl.when(row + u < rows)
         def _():
             for c in early:
-                await_up(u, c)
+                if u > 1:
+                    await_up(u, c)
+                else:
+
+                    @pl.when(row != gate_low)
+                    def _():
+                        await_up(u, c)
+
                 if u > 1:
                     up(0, u, c).start()
                 else:
@@ -328,7 +349,6 @@
     lax.fori_loop(0, pairs, one_pair, 0)
 
     results = ((attended_own, attended_out), (scores_own, scores_all))
-    half = rows // 2
     low = row < half
 
     def along(i, u):
@@ -448,7 +468,7 @@
 
 
 def settle(n, pieces, keys, values, attended, scores, *rest):
-    cache_keys, cache_values, attended_out, scores_out, sems = rest
+    cache_keys, cache_values, attended_out, scores_out, turned_scores, sems = rest
     me = lax.axis_index("seq")
     here = scores_out.shape[0]
     step = keys.shape[0] // pieces
@@ -464,7 +484,9 @@
         store.start()
     flat = scores[...].reshape(math.prod(scores.shape[:-1]), BLOCK)
     turned = pltpu.roll(flat, lax.rem(BLOCK - me * here, BLOCK), 1)
-    scores_out[...] = turned.T[:here]
+    turned_scores[...] = turned.T[:here]
+    stores.append(pltpu.make_async_copy(turned_scores, scores_out, sems.at[len(stores)]))
+    stores[-1].start()
     for store in stores:
         store.wait()
 
@@ -528,8 +550,11 @@
             jax.ShapeDtypeStruct((part // BLOCK, every), f32),
         ),
         in_specs=[vmem] * 4,
-        out_specs=(free, free, free, vmem),
-        scratch_shapes=[pltpu.SemaphoreType.DMA((2 * pieces + 1,))],
+        out_specs=(free,) * 4,
+        scratch_shapes=[
+            pltpu.VMEM((part // BLOCK, every), f32),
+            pltpu.SemaphoreType.DMA((2 * pieces + 2,)),
+        ],
         compiler_params=pltpu.CompilerParams(vmem_limit_bytes=LIMIT),
     )(*moved)
     return cache_keys, cache_values, attended.reshape((every,) + queries.shape[1:]), scores.T

time: 194 us -> 192 us (0.990)
  no operation moved by 1% of the time
where the time goes in v3:
time: 192 us
  Pallas kernels  192 us (100%)
    pallas_call x1, Pallas kernels, local(): pl.pallas_call(functools.partial(kernel, n, min(512, tokens), inner), out...  188 us

profile of v3, /device:TPU:19, one launch (start us, length us, event | category | flops | bytes accessed | tf_op | source)
XLA Modules:
  0.0 192.2 jit_solution(7865842809784343437)
XLA Ops:
  0.6 188.0 %shard_map.111 = (bf16[64,256,128]{2,1,0:T(8,128)(2,1)S(1)}, bf16[64,256,128]{2,1,0:T(8,128)(2,1)S(1)}, bf16[4,4,4,2,8,128]{5,4,3,2,1,0:T(8,128)(2,1)S(1)}, f32[4,4,4,128]{3,2,1,0:T(4,128)S(1)}) custom-call(bf16[4,4096,128]{2,1,0:T(8,128)(2,1)} %keys_hbm.1, bf16[4,4096,128]{2,1,0:T(8,128)(2,1)} %values_hbm.1, bf16[4,8,256,128]{3,2,1,0:T(8,128)(2,1)} %window_hbm.1, ...), custom_call_target="tpu_custom_call" | custom-call | tf_op jit(solution)/shard_map/pallas_call | solution.py:506
  188.7 3.5 %shard_map.112 = (bf16[64,256,128]{2,1,0:T(8,128)(2,1)}, bf16[64,256,128]{2,1,0:T(8,128)(2,1)}, bf16[4,4,4,2,8,128]{5,4,3,2,1,0:T(8,128)(2,1)}, f32[2,64]{1,0:T(2,128)}) custom-call(bf16[64,256,128]{2,1,0:T(8,128)(2,1)S(1)} %get-tuple-element.12.keys, bf16[64,256,128]{2,1,0:T(8,128)(2,1)S(1)} %get-tuple-element.13.values, ...), custom_call_target="tpu_custom_call" | custom-call | tf_op jit(solution)/shard_map/pallas_call | solution.py:544

commit v4 on v3

--- a/solution.py
+++ b/solution.py
@@ -172,6 +172,10 @@
     def await_up(distance, c):
         pl.semaphore_wait(present.at[(row + distance) * inner + (column ^ c)], 1)
 
+    @pl.when((row > 1) & (row == gate_high))
+    def _():
+        start_down(row - 1, (0,))
+
     @pl.when(row > 0)
     def _():
         start_down(row, (0, 1))
@@ -182,7 +186,7 @@
         def _():
             start_down(u, (0, 1))
 
-        @pl.when(u == row - 1)
+        @pl.when((u == row - 1) & (row != gate_high))
         def _():
             start_down(u, (0,))
 
@@ -540,7 +544,7 @@
             collective_id=0, has_side_effects=True, vmem_limit_bytes=LIMIT
         ),
     )(*(pltpu.with_memory_space_constraint(a, pltpu.HBM) for a in args))
-    pieces = math.gcd(every, 8)
+    pieces = math.gcd(every, 2)
     cache_keys, cache_values, attended, scores = pl.pallas_call(
         functools.partial(settle, n, pieces),
         out_shape=(

time: 192 us -> 192 us (level)
  no operation moved by 1% of the time
where the time goes in v4:
time: 192 us
  Pallas kernels  191 us (99%)
    pallas_call x1, Pallas kernels, local(): pl.pallas_call(functools.partial(kernel, n, min(512, tokens), inner), out...  188 us

profile of v4, /device:TPU:19, one launch (start us, length us, event | category | flops | bytes accessed | tf_op | source)
XLA Modules:
  0.0 192.1 jit_solution(1403889542292164806)
XLA Ops:
  0.6 188.0 %shard_map.111 = (bf16[64,256,128]{2,1,0:T(8,128)(2,1)S(1)}, bf16[64,256,128]{2,1,0:T(8,128)(2,1)S(1)}, bf16[4,4,4,2,8,128]{5,4,3,2,1,0:T(8,128)(2,1)S(1)}, f32[4,4,4,128]{3,2,1,0:T(4,128)S(1)}) custom-call(bf16[4,4096,128]{2,1,0:T(8,128)(2,1)} %keys_hbm.1, bf16[4,4096,128]{2,1,0:T(8,128)(2,1)} %values_hbm.1, bf16[4,8,256,128]{3,2,1,0:T(8,128)(2,1)} %window_hbm.1, ...), custom_call_target="tpu_custom_call" | custom-call | tf_op jit(solution)/shard_map/pallas_call | solution.py:510
  188.7 3.4 %shard_map.112 = (bf16[64,256,128]{2,1,0:T(8,128)(2,1)}, bf16[64,256,128]{2,1,0:T(8,128)(2,1)}, bf16[4,4,4,2,8,128]{5,4,3,2,1,0:T(8,128)(2,1)}, f32[2,64]{1,0:T(2,128)}) custom-call(bf16[64,256,128]{2,1,0:T(8,128)(2,1)S(1)} %get-tuple-element.12.keys, bf16[64,256,128]{2,1,0:T(8,128)(2,1)S(1)} %get-tuple-element.13.values, ...), custom_call_target="tpu_custom_call" | custom-call | tf_op jit(solution)/shard_map/pallas_call | solution.py:548
